TPU v7x, 128 devices: a whole 4x4x4 slice. The times are simulated.
128 devices in a mesh: prow: 16 (over y, x), pcol: 8 (over z, core).
Axes of the slice: x: 4, y: 4, z: 4, core: 2. Of those that a mesh axis runs over, the one named last changes fastest.
Arguments:
- u_window: float32 [6, 16, 512, 4, 8, 512], P(None, 'prow', None, None, 'pcol'), may hold values from -0.5 to 0.5
Outputs:
- lauum_columns: float32 [1024, 6, 16, 512], P('pcol', None, 'prow')
All inputs are finite; a program needn't handle non-finite values.
Results may differ from a plain program's by a relative error of at most 0.000061.
Values sent between devices are 32-bit elements; how exact they have to be, the bound alone decides.
A program may use at most 192 MiB of HBM per device.

v0:
```python
import jax
import jax.numpy as jnp
from jax import lax
from jax.sharding import PartitionSpec as P


def broadcast(value, axis, source):
    kept = jnp.where(lax.axis_index(axis) == source, value, 0).astype(value.dtype)
    return lax.psum(kept, axis)


def contract(left, right):
    return lax.dot_general(
        left,
        right,
        (((1,), (1,)), ((), ())),
        precision=lax.Precision.HIGHEST,
        preferred_element_type=jnp.float32,
    )


def on_device(u_window):
    row_blocks = u_window.shape[0]
    block_size = u_window.shape[2]
    col_blocks = u_window.shape[3]
    prow_size = lax.axis_size("prow")
    pcol_size = lax.axis_size("pcol")
    my_row = lax.axis_index("prow")
    my_col = lax.axis_index("pcol")
    blocks = u_window.reshape(row_blocks * block_size, col_blocks * block_size)
    last_row = blocks[(row_blocks - 1) * block_size :]
    anchor = (row_blocks * prow_size - 2) * block_size
    row_ids = ((row_blocks - 1) * prow_size + my_row) * block_size + jnp.arange(
        block_size, dtype=jnp.int32
    )
    col_index = jnp.arange(col_blocks * block_size, dtype=jnp.int32)
    window_col = (
        col_index // block_size * pcol_size + my_col
    ) * block_size + col_index % block_size
    masked = jnp.where(
        row_ids[:, None] <= anchor + window_col[None, :], last_row, jnp.zeros_like(last_row)
    )
    first_panel = broadcast(masked, "prow", prow_size - 2)
    second_panel = broadcast(masked, "prow", prow_size - 1)
    panels = jnp.concatenate([first_panel, second_panel], 0)
    top_rows = blocks[: (row_blocks - 1) * block_size]
    ending = contract(panels, masked)
    summed = lax.psum_scatter(
        jnp.concatenate([contract(panels, top_rows), ending], 1),
        "pcol",
        scatter_dimension=0,
        tiled=True,
    )
    share_rows = summed.shape[0]
    return summed.reshape(share_rows, row_blocks, 1, block_size)


def solution(mesh):
    placed = (P(None, "prow", None, None, "pcol", None),)
    return jax.shard_map(
        on_device,
        mesh=mesh,
        in_specs=placed,
        out_specs=P("pcol", None, "prow", None),
        check_vma=False,
    )
```

profile of v0, /device:TPU:0, one launch (start us, length us, event | category | flops | bytes accessed | tf_op | source)
XLA Modules:
  0.0 367.3 jit_solution(13802270295498599830)
XLA Ops:
  6.5 0.0 all-reduce.3.cloned.1.call-start
  6.6 12.9 %slice_reduce_fusion.1 = f32[512,4,512]{2,1,0:T(4,128)S(1)} fusion(f32[6,1,512,4,1,512]{5,4,3,2,1,0:T(1,128)} %param.1), kind=kLoop, calls=%fused_computation.2 | loop fusion | bytes 8388608 | tf_op jit(solution)/shard_map/slice | solution.py:31
  19.4 2.0 copy.8
  21.4 0.0 copy-start
  21.4 4.3 %fusion.1 = (f32[512,2048]{1,0:T(8,128)}, f32[512,2048]{1,0:T(8,128)}) fusion(f32[512,2048]{1,0:T(8,128)S(1)} %bitcast.13, s32[2048]{0:T(1024)S(1)} %fusion.16, s32[512]{0:T(512)S(1)} %iota_add_fusion, pred[]{:T(512)S(6)} %eq.9, pred[]{:T(512)S(6)} %eq.8), kind=kLoop, calls=%fused_computation.5 | loop fusion | flops 4194304 | bytes 12593154 | tf_op jit(solution)/shard_map/jit(_where)/select_n | solution.py:8
  25.7 0.2 copy-done
  25.9 0.0 all-reduce.3.cloned.1.call-update
  26.0 0.2 reduce-scatter.2.cloned.1.call-start
  26.2 67.3 %slice_reduce_fusion = f32[5,512,4,512]{3,2,1,0:T(4,128)} fusion(f32[6,1,512,4,1,512]{5,4,3,2,1,0:T(1,128)} %param.1), kind=kLoop, calls=%fused_computation | loop fusion | bytes 41943040 | tf_op jit(solution)/shard_map/slice | solution.py:46
  93.4 21.1 %copy.9 = f32[320,8,4,512]{3,1,2,0:T(8,128)} copy(f32[320,8,4,512]{3,2,1,0:T(4,128)} %bitcast.9) | data formatting | bytes 41943040
  114.5 55.7 %all-reduce.3.cloned.1.call-done = (f32[512,2048]{1,0:T(8,128)}, f32[512,2048]{1,0:T(8,128)}) async-done(((f32[512,2048]{1,0:T(8,128)}, f32[512,2048]{1,0:T(8,128)}), (f32[512,2048]{1,0:T(8,128)}, f32[512,2048]{1,0:T(8,128)})) %all-reduce.3.cloned.1.call-update) | async-done | bytes 8388624 | tf_op jit(solution)/shard_map/psum | solution.py:9
  170.2 0.0 slice-start
  170.2 0.0 slice-start.1
  170.2 5.0 %constant_dynamic-update-slice_fusion.1 = f32[1024,2048]{1,0:T(8,128)} fusion(f32[512,2048]{1,0:T(8,128)} %get-tuple-element.5), kind=kLoop, calls=%fused_computation.27 | loop fusion | bytes 8388608
  175.2 0.0 copy-start.1
  175.2 0.0 slice-start.2
  175.2 5.2 %constant_dynamic-update-slice_fusion = f32[1024,2048]{1,0:T(8,128)} fusion(f32[1024,2048]{1,0:T(8,128)} %constant_dynamic-update-slice_fusion.1, f32[512,2048]{1,0:T(8,128)} %get-tuple-element.6), kind=kLoop, calls=%fused_computation.26 | loop fusion | bytes 8388608 | tf_op jit(solution)/shard_map/concatenate | solution.py:45
  180.3 0.0 copy-done.1
  180.3 0.0 slice-start.3
  180.3 0.0 slice-start.4
  180.3 18.1 %fusion = f32[1024,512]{1,0:T(8,128)} fusion(f32[1024,2048]{1,0:T(8,128)} %constant_dynamic-update-slice_fusion, f32[512,2048]{1,0:T(8,128)S(1)} %bitcast.14, s32[2048]{0:T(1024)S(1)} %fusion.16, s32[512]{0:T(512)S(1)} %iota_add_fusion), kind=kOutput, calls=%fused_computation.4 | convolution fusion | flops 12886999040 | bytes 14690304 | tf_op jit(solution)/shard_map/dot_general | solution.py:13
  198.5 0.0 slice-done
  198.5 0.0 slice-done.1
  198.5 0.0 slice-done.2
  198.5 0.0 slice-done.3
  198.5 0.0 slice-done.4
  198.5 75.4 %fusion.19 = f32[1024,2560]{1,0:T(8,128)} fusion(f32[1024,2048]{1,0:T(8,128)} %constant_dynamic-update-slice_fusion, f32[2560,2048]{1,0:T(8,128)S(1)} %bitcast.12), kind=kOutput, calls=%fused_computation.30 | convolution fusion | flops 64424509440 | bytes 39845888 | tf_op jit(solution)/shard_map/dot_general | solution.py:13
  273.9 10.2 %pad_maximum_fusion = f32[1024,3072]{1,0:T(8,128)} fusion(f32[1024,512]{1,0:T(8,128)} %fusion, f32[1024,2560]{1,0:T(8,128)} %fusion.19), kind=kLoop, calls=%fused_computation.1 | loop fusion | flops 3145728 | bytes 25165824 | tf_op jit(solution)/shard_map/concatenate | solution.py:49
  284.1 0.0 reduce-scatter.2.cloned.1.call-update
  284.1 71.7 %reduce-scatter.2.cloned.1.call-done = f32[128,3072]{1,0:T(8,128)} async-done(((f32[1024,3072]{1,0:T(8,128)}), f32[128,3072]{1,0:T(8,128)}) %reduce-scatter.2.cloned.1.call-update) | async-done | bytes 1572880 | tf_op jit(solution)/shard_map/reduce_scatter | solution.py:48
  355.8 1.9 copy.5
  357.7 2.7 copy.6
  (3 shorter events, 0.0 us)
Async XLA Ops:
  6.5 163.7 %all-reduce.3.cloned.1.call-start = ((), (), s32[]{:S(2)}) async-start(), calls=%async_computation.2 | async-start | bytes 16777216 | tf_op jit(solution)/shard_map/psum | solution.py:9
  21.4 4.5 %copy-start = (f32[64,8,4,512]{3,1,2,0:T(8,128)}, f32[64,8,4,512]{3,1,2,0:T(8,128)S(1)}, u32[]{:S(2)}) copy-start(f32[64,8,4,512]{3,1,2,0:T(8,128)S(1)} %copy.8) | copy-start | bytes 12582916
  26.0 329.9 %reduce-scatter.2.cloned.1.call-start = ((), (), s32[]{:S(2)}) async-start(), calls=%async_computation.1 | async-start | bytes 14155776 | tf_op jit(solution)/shard_map/reduce_scatter | solution.py:48
  170.2 28.3 %slice-start = ((s8[20971520]{0:T(1024)(128)(4,1)}), s8[4194304]{0:T(1024)(128)(4,1)S(1)}, s32[]{:S(2)}) async-start(s8[20971520]{0:T(1024)(128)(4,1)} %bitcast.10), calls=%async_computation.3 | async-start | bytes 8388608
  170.2 28.3 %slice-start.1 = ((s8[20971520]{0:T(1024)(128)(4,1)}), s8[4194304]{0:T(1024)(128)(4,1)S(1)}, s32[]{:S(2)}) async-start(s8[20971520]{0:T(1024)(128)(4,1)} %bitcast.10), calls=%async_computation.4 | async-start | bytes 8388608
  175.2 5.2 %copy-start.1 = (f32[64,8,4,512]{3,1,2,0:T(8,128)S(1)}, f32[64,8,4,512]{3,1,2,0:T(8,128)}, u32[]{:S(2)}) copy-start(f32[64,8,4,512]{3,1,2,0:T(8,128)} %copy-done) | copy-start | bytes 12582916
  175.2 23.3 %slice-start.2 = ((s8[20971520]{0:T(1024)(128)(4,1)}), s8[4194304]{0:T(1024)(128)(4,1)S(1)}, s32[]{:S(2)}) async-start(s8[20971520]{0:T(1024)(128)(4,1)} %bitcast.10), calls=%async_computation.5 | async-start | bytes 8388608
  180.3 18.1 %slice-start.3 = ((s8[20971520]{0:T(1024)(128)(4,1)}), s8[4194304]{0:T(1024)(128)(4,1)S(1)}, s32[]{:S(2)}) async-start(s8[20971520]{0:T(1024)(128)(4,1)} %bitcast.10), calls=%async_computation.6 | async-start | bytes 8388608
  180.3 18.1 %slice-start.4 = ((s8[20971520]{0:T(1024)(128)(4,1)}), s8[4194304]{0:T(1024)(128)(4,1)S(1)}, s32[]{:S(2)}) async-start(s8[20971520]{0:T(1024)(128)(4,1)} %bitcast.10), calls=%async_computation.7 | async-start | bytes 8388608
Sparse Core Ops, SparseCore 0:
  26.1 144.0 all-reduce.2
  284.2 71.5 reduce-scatter.1
where the time goes:
time: 368 us; the launch traced here: 367 us
  waiting for transfers between devices  127 us (35%)
  local copies, waits for them, and re-layouts  118 us (32%)
  matrix products  93.5 us (25%)
  other arithmetic  14.5 us (4%)
  between operations  13.5 us (4%)
    dot_general x2, matrix products, contract(): lax.dot_general(left, right, (((1,), (1,)), ((), ())), precision=lax.Prec...  93.5 us
    reduce_scatter x1, waiting for transfers between devices, on_device(): lax.psum_scatter(jnp.concatenate([contract(panels, top_rows), ending], 1)...  71.7 us
    slice x1, local copies, waits for them, and re-layouts, on_device(): top_rows = blocks[:(row_blocks - 1) * block_size]  67.3 us
    psum x1, waiting for transfers between devices, broadcast(): return lax.psum(kept, axis)  55.7 us
    unnamed x17, local copies, waits for them, and re-layouts  28.3 us
    slice x1, local copies, waits for them, and re-layouts, on_device(): last_row = blocks[(row_blocks - 1) * block_size:]  12.9 us
    concatenate x1, other arithmetic, on_device(): jnp.concatenate([contract(panels, top_rows), ending], 1)  10.2 us
  transfers between devices with their start and end apart: 2, of which 2 were waited for; matrix products, arithmetic and copies ran while one was open for 24% of the time, Pallas kernels for 0%

commit v1 on v0

v1 whole, which is shorter than its diff:
```python
import functools

import jax
import jax.numpy as jnp
from jax import lax
from jax.experimental import pallas as pl
from jax.experimental.pallas import tpu as pltpu
from jax.sharding import PartitionSpec as P

MESH = pl.DeviceIdType.MESH
ROWS = 16
SPLIT = 2
SLOTS = 3
LAG = 4


def gray(index):
    return index ^ (index >> 1)


def address(row):
    return gray(row // 4) * 4 + gray(row % 4)


def parents(tree):
    order = [(tree + k + 1) % 4 for k in range(4)]
    order = ([(tree - k - 1) % 4 for k in range(4)])[::-1]
    found = {}
    for node in range(1, 16):
        rest = node ^ (1 << tree)
        found[node] = 0 if rest == 0 else node ^ (1 << [d for d in order if rest >> d & 1][0])
    return found


def plans(n_rows, sources):
    trees = [parents(tree) for tree in range(4)]
    taken = set()
    for tree in trees:
        for node, parent in tree.items():
            assert (parent, node) not in taken
            taken.add((parent, node))
    result = []
    for row in range(n_rows):
        pieces = []
        for index, source in enumerate(sources):
            me = address(row) ^ address(source)
            for number, tree in enumerate(trees):
                depth, node = 0, me
                while node:
                    depth, node = depth + 1, tree[node]
                mask = sum(1 << d for d in range(4) if tree.get(me ^ (1 << d)) == me)
                pieces.append((depth, index * 4 + number, mask))
        result.append(sorted(pieces))
    return result


def kernel(
    x_ref,
    out_ref,
    high,
    low,
    panel,
    left,
    part,
    fold,
    mid,
    last,
    stage,
    in_sem,
    go_sem,
    fold_send,
    fold_recv,
    mid_send,
    mid_recv,
    last_send,
    last_recv,
    out_sem,
    stage_sem,
    *,
    n_row,
    n_col,
):
    p = lax.axis_index("prow")
    q = lax.axis_index("pcol")
    z, c = q // 2, q % 2
    n_block, depth, block = high.shape
    lanes = depth // 128
    per_block = block // 128
    n_stage = n_block * per_block
    n_set = panel.shape[0]
    n_step = n_set * SPLIT
    width = part.shape[2]
    half = part.shape[1] // 2
    first_source = n_row - 2
    anchor = n_row * n_block - 2

    x, y = p % 4, p // 4
    near = [
        y * 4 + x + 1 - 2 * (x % 2),
        y * 4 + 3 - x,
        (y + 1 - 2 * (y % 2)) * 4 + x,
        (3 - y) * 4 + x,
    ]
    peer = q + 1 - 2 * c
    up = ((z + 1) % 4) * 2 + c
    down = ((z + 3) % 4) * 2 + c

    def pick(values):
        found = jnp.int32(values[0])
        for k in range(1, n_row):
            found = jnp.where(p == k, jnp.int32(values[k]), found)
        return found

    plan = plans(n_row, (first_source, first_source + 1))
    routes = [
        pick([sum((e[1] + 8 * e[2]) << 7 * k for k, e in enumerate(row[g : g + 4])) for row in plan])
        for g in (0, 4)
    ]
    depths = [
        pick([sum(e[0] << 3 * k for k, e in enumerate(row[g : g + 4])) for row in plan])
        for g in (0, 4)
    ]

    def place(piece):
        return pl.multiple_of(((piece % 2) * 4 + piece // 2) * (ROWS * lanes), ROWS * lanes)

    def piece_ref(s, piece):
        return panel.at[s, pl.ds(place(piece), ROWS * lanes), :]

    def stage_copy(n):
        slot = n % SLOTS
        return pltpu.make_async_copy(
            x_ref.at[pl.ds(pl.multiple_of(n * (128 * lanes), 128 * lanes), 128 * lanes), :],
            stage.at[slot],
            stage_sem.at[slot],
        )

    for n in range(SLOTS):
        stage_copy(n).start()

    @pl.when(p >= first_source)
    def _():
        def own(s, _):
            for t in range(4):
                piece = (p - first_source) * 4 + t
                row = (n_block - 1) * block + t * 128 + s * ROWS
                pltpu.make_async_copy(
                    x_ref.at[pl.ds(pl.multiple_of(row * lanes, ROWS * lanes), ROWS * lanes), :],
                    piece_ref(s, piece),
                    in_sem.at[s, piece],
                ).start()
            return 0

        lax.fori_loop(0, n_set, own, 0)

    barrier = pltpu.get_barrier_semaphore()
    partners = [(row, q) for row in near] + [(p, peer), (p, up), (p, down)]
    for partner in partners:
        pl.semaphore_signal(barrier, inc=1, device_id=partner, device_id_type=MESH)
    pl.semaphore_wait(barrier, len(partners))

    def prepare(n, _):
        slot = n % SLOTS
        stage_copy(n).wait()
        row_id = (
            ((n // per_block) * n_row + p - anchor) * block
            + (n % per_block) * 128
            + lax.broadcasted_iota(jnp.int32, (128, 128), 1)
        )
        for j in range(lanes):
            value = stage[slot, pl.ds(j, 128, stride=lanes), :].T
            first_col = (j // per_block * n_col + q) * block + j % per_block * 128
            if j < per_block:
                col_id = first_col + lax.broadcasted_iota(jnp.int32, (128, 128), 0)
                value = jnp.where(row_id <= col_id, value, 0.0)
            top = value.astype(jnp.bfloat16)
            at = (n // per_block, pl.ds(j * 128, 128), pl.ds(pl.multiple_of(n % per_block * 128, 128), 128))
            high[at] = top
            low[at] = (value - top.astype(jnp.float32)).astype(jnp.bfloat16)

        @pl.when(n + SLOTS < n_stage)
        def _():
            stage_copy(n + SLOTS).start()

        return 0

    def relay(s, done, pace):
        for group in range(2):

            def one(j, carry):
                route, far, done = carry
                piece, mask = route % 8, route // 8 % 16
                if pace:
                    goal = jnp.minimum(far % 8 * pace, n_stage)
                    goal = jnp.maximum(goal, done)
                    lax.fori_loop(done, goal, prepare, 0)
                    done = goal
                ref = piece_ref(s, piece)
                pltpu.make_async_copy(ref, ref, in_sem.at[s, piece]).wait()
                for d in range(4):

                    @pl.when(mask // (1 << d) % 2 == 1)
                    def _():
                        slot = go_sem.at[group * 4 + j, d]

                        @pl.when(s > 0)
                        def _():
                            pltpu.make_async_copy(ref, ref, slot).wait()

                        pltpu.make_async_remote_copy(
                            src_ref=ref,
                            dst_ref=ref,
                            send_sem=slot,
                            recv_sem=in_sem.at[s, piece],
                            device_id=(near[d], q),
                            device_id_type=MESH,
                        ).start()

                return route // 128, far // 8, done

            done = lax.fori_loop(0, 4, one, (routes[group], depths[group], done))[2]
        return done

    def split_panel(s):
        row = lax.broadcasted_iota(jnp.int32, (8 * ROWS, 128), 0)
        place_of, within = row // ROWS, row % ROWS
        row_id = (place_of % 4 * 2 + place_of // 4) * 128 + s * ROWS + within
        for j in range(lanes):
            value = panel[s, pl.ds(j, 8 * ROWS, stride=lanes), :]
            if j < per_block:
                col_id = q * block + j * 128 + lax.broadcasted_iota(jnp.int32, (8 * ROWS, 128), 1)
                value = jnp.where(row_id <= col_id, value, 0.0)
            top = value.astype(jnp.bfloat16)
            left[: 8 * ROWS, j * 128 : j * 128 + 128] = top
            left[8 * ROWS :, j * 128 : j * 128 + 128] = (value - top.astype(jnp.float32)).astype(
                jnp.bfloat16
            )

    def fold_copy(t):
        return pltpu.make_async_remote_copy(
            src_ref=part.at[t, pl.ds(pl.multiple_of((1 - c) * half, half), half), :],
            dst_ref=fold.at[t],
            send_sem=fold_send.at[t],
            recv_sem=fold_recv.at[t],
            device_id=(p, peer),
            device_id_type=MESH,
        )

    def rows_of(zone, offset):
        return pl.multiple_of(c * half + zone * ROWS + offset, 8)

    def mid_copy(t, way):
        start = rows_of((z + 2) % 4, way * (ROWS // 2))
        return pltpu.make_async_remote_copy(
            src_ref=part.at[t, pl.ds(start, ROWS // 2), :],
            dst_ref=mid.at[t, way],
            send_sem=mid_send.at[t, way],
            recv_sem=mid_recv.at[t, way],
            device_id=(p, (up, down)[way]),
            device_id_type=MESH,
        )

    def last_copy(t, way):
        start = rows_of((z + (1, 3)[way]) % 4, 0)
        return pltpu.make_async_remote_copy(
            src_ref=part.at[t, pl.ds(start, ROWS), :],
            dst_ref=last.at[t, way],
            send_sem=last_send.at[t, way],
            recv_sem=last_recv.at[t, way],
            device_id=(p, (up, down)[way]),
            device_id_type=MESH,
        )

    def out_copy(t):
        return pltpu.make_async_copy(
            part.at[t, pl.ds(rows_of(z, 0), ROWS), :],
            out_ref.at[
                pl.ds(pl.multiple_of(t // SPLIT * ROWS, ROWS), ROWS),
                pl.ds(pl.multiple_of(t % SPLIT * width, width), width),
            ],
            out_sem.at[t],
        )

    def compute(t):
        s, h = t // SPLIT, t % SPLIT
        for i in range(n_block // SPLIT):
            at = h * (n_block // SPLIT) + i
            both = jnp.dot(left[...], high[at], preferred_element_type=jnp.float32)
            rest = jnp.dot(left[: 8 * ROWS], low[at], preferred_element_type=jnp.float32)
            part[t, :, i * block : (i + 1) * block] = both[: 8 * ROWS] + both[8 * ROWS :] + rest

    def add_fold(t):
        fold_copy(t).wait_recv()
        for r in range(0, half, 8):
            at = (t, pl.ds(pl.multiple_of(c * half + r, 8), 8), slice(None))
            part[at] = part[at] + fold[t, r : r + 8, :]
        for way in range(2):
            mid_copy(t, way).start()

    def add_mid(t):
        for way in range(2):
            mid_copy(t, way).wait_recv()
            at = (t, pl.ds(rows_of((z + (1, 3)[way]) % 4, way * (ROWS // 2)), ROWS // 2), slice(None))
            part[at] = part[at] + mid[t, way]
        for way in range(2):
            last_copy(t, way).start()

    def add_last(t):
        for way in range(2):
            last_copy(t, way).wait_recv()
        for r in range(0, ROWS, 8):
            at = (t, pl.ds(rows_of(z, r), 8), slice(None))
            part[at] = part[at] + last[t, 0, r : r + 8, :] + last[t, 1, r : r + 8, :]
        out_copy(t).start()

    done = relay(0, jnp.int32(0), 8)
    lax.fori_loop(done, n_stage, prepare, 0)

    def step(t, _):
        @pl.when(t < n_step)
        def _():
            @pl.when(t % SPLIT == 0)
            def _():
                s = t // SPLIT

                @pl.when(s > 0)
                def _():
                    relay(s, jnp.int32(0), 0)

                split_panel(s)

            compute(t)
            fold_copy(t).start()

        for lag, work in ((1, add_fold), (2, add_mid), (LAG, add_last)):

            @pl.when((t >= lag) & (t < n_step + lag))
            def _():
                work(t - lag)

        return 0

    lax.fori_loop(0, n_step + LAG, step, 0)

    def finish(t, _):
        fold_copy(t).wait_send()
        for way in range(2):
            mid_copy(t, way).wait_send()
            last_copy(t, way).wait_send()
        out_copy(t).wait()
        return 0

    lax.fori_loop(0, n_step, finish, 0)
    for group in range(2):

        def spent(j, route):
            ref = piece_ref(0, route % 8)
            for d in range(4):

                @pl.when(route // 8 % 16 // (1 << d) % 2 == 1)
                def _():
                    pltpu.make_async_copy(ref, ref, go_sem.at[group * 4 + j, d]).wait()

            return route // 128

        lax.fori_loop(0, 4, spent, routes[group])


def on_device(u_window):
    n_block, _, block, col_blocks, _, _ = u_window.shape
    n_row, n_col = lax.axis_size("prow"), lax.axis_size("pcol")
    depth = col_blocks * block
    lanes = depth // 128
    height = n_block * block
    width = height // SPLIT
    n_set = 128 // ROWS
    n_step = n_set * SPLIT
    dma = pltpu.SemaphoreType.DMA
    summed = pl.pallas_call(
        functools.partial(kernel, n_row=n_row, n_col=n_col),
        out_shape=jax.ShapeDtypeStruct((2 * block // n_col, height), jnp.float32),
        in_specs=[pl.BlockSpec(memory_space=pl.ANY)],
        out_specs=pl.BlockSpec(memory_space=pl.ANY),
        scratch_shapes=[
            pltpu.VMEM((n_block, depth, block), jnp.bfloat16),
            pltpu.VMEM((n_block, depth, block), jnp.bfloat16),
            pltpu.VMEM((n_set, 8 * ROWS * lanes, 128), jnp.float32),
            pltpu.VMEM((16 * ROWS, depth), jnp.bfloat16),
            pltpu.VMEM((n_step, 8 * ROWS, width), jnp.float32),
            pltpu.VMEM((n_step, 4 * ROWS, width), jnp.float32),
            pltpu.VMEM((n_step, 2, ROWS // 2, width), jnp.float32),
            pltpu.VMEM((n_step, 2, ROWS, width), jnp.float32),
            pltpu.VMEM((SLOTS, 128 * lanes, 128), jnp.float32),
            dma((n_set, 8)),
            dma((8, 4)),
            dma((n_step,)),
            dma((n_step,)),
            dma((n_step, 2)),
            dma((n_step, 2)),
            dma((n_step, 2)),
            dma((n_step, 2)),
            dma((n_step,)),
            dma((SLOTS,)),
        ],
        compiler_params=pltpu.CompilerParams(
            collective_id=0, has_side_effects=True, vmem_limit_bytes=67043328
        ),
    )(u_window.reshape(height * lanes, 128))
    return summed.reshape(summed.shape[0], n_block, 1, block)


def solution(mesh):
    placed = (P(None, "prow", None, None, "pcol", None),)
    return jax.shard_map(
        on_device,
        mesh=mesh,
        in_specs=placed,
        out_specs=P("pcol", None, "prow", None),
        check_vma=False,
    )
```

time: 368 us -> 205 us (0.56)
  Pallas kernels: 0 us -> 200 us
  waiting for transfers between devices: 127 us -> 0 us
  local copies, waits for them, and re-layouts: 118 us -> 4.61 us
  matrix products: 93.5 us -> 0 us
  other arithmetic: 14.5 us -> 0 us
  between operations: 13.5 us -> 0.02 us
    pallas_call x0 -> x1, Pallas kernels: none -> 200 us  [on_device(): pl.pallas_call(functools.partial(kernel, n_row=n_row, n_col=n_col), out_s...]
    dot_general x2 -> x0, matrix products: 93.5 us -> none  [contract(): lax.dot_general(left, right, (((1,), (1,)), ((), ())), precision=lax.Prec...]
    slice x2 -> x0, local copies, waits for them, and re-layouts: 80.1 us -> none  [the longest x1 67.3 us: on_device(): top_rows = blocks[:(row_blocks - 1) * block_size]]
    reduce_scatter x1 -> x0, waiting for transfers between devices: 71.7 us -> none  [on_device(): lax.psum_scatter(jnp.concatenate([contract(panels, top_rows), ending], 1)...]
    psum x1 -> x0, waiting for transfers between devices: 55.7 us -> none  [broadcast(): return lax.psum(kept, axis)]
    unnamed x17 -> x0, local copies, waits for them, and re-layouts: 28.3 us -> none
    concatenate x1 -> x0, other arithmetic: 10.2 us -> none  [on_device(): jnp.concatenate([contract(panels, top_rows), ending], 1)]
    concatenate x1 -> x0, local copies, waits for them, and re-layouts: 5.18 us -> none  [on_device(): panels = jnp.concatenate([first_panel, second_panel], 0)]
  transfers between devices with their start and end apart: 2 -> 0, of which waited for: 2 -> 0; matrix products, arithmetic and copies ran while one was open for 24% -> 0% of each run, Pallas kernels for 0% -> 0%
where the time goes in v1:
time: 205 us
  Pallas kernels  200 us (98%)
  local copies, waits for them, and re-layouts  4.61 us (2%)
    pallas_call x1, Pallas kernels, on_device(): pl.pallas_call(functools.partial(kernel, n_row=n_row, n_col=n_col), out_s...  200 us

profile of v1, /device:TPU:0, one launch (start us, length us, event | category | flops | bytes accessed | tf_op | source)
XLA Modules:
  0.0 205.0 jit_solution(5981606587271059929)
XLA Ops:
  0.0 200.3 %shard_map.17 = f32[128,3072]{1,0:T(8,128)} custom-call(f32[49152,128]{1,0:T(8,128)} %bitcast.2), custom_call_target="tpu_custom_call" | custom-call | tf_op jit(solution)/shard_map/pallas_call | solution.py:379
  200.3 1.9 copy.3
  202.2 2.7 %copy.4 = f32[128,6,1,512]{3,2,1,0:T(1,128)} copy(f32[128,6,1,512]{0,3,1,2:T(8,128)S(1)} %bitcast.3) | data formatting | bytes 3145728 | tf_op jit(solution)/shard_map/reshape | solution.py:409

commit v2 on v1

v2 whole, which is shorter than its diff:
```python
import functools

import jax
import jax.numpy as jnp
from jax import lax
from jax.experimental import pallas as pl
from jax.experimental.pallas import tpu as pltpu
from jax.sharding import PartitionSpec as P

MESH = pl.DeviceIdType.MESH
ROWS = 16
PIECE = 8
TURNS = 3
DELAY = (0, 4, 8, 12, 16, 20)
SPLIT = 2
SLOTS = 3
LAGS = (1, 2, 4)


def gray(index):
    return index ^ (index >> 1)


def address(row):
    return gray(row // 4) * 4 + gray(row % 4)


def parents(tree):
    order = [(tree + k + 1) % 4 for k in range(4)]
    order = ([(tree - k - 1) % 4 for k in range(4)])[::-1]
    found = {}
    for node in range(1, 16):
        rest = node ^ (1 << tree)
        found[node] = 0 if rest == 0 else node ^ (1 << [d for d in order if rest >> d & 1][0])
    return found


def plans(n_rows, sources):
    trees = [parents(tree) for tree in range(4)]
    taken = set()
    for tree in trees:
        for node, parent in tree.items():
            assert (parent, node) not in taken
            taken.add((parent, node))
    result = []
    for row in range(n_rows):
        pieces = []
        for index, source in enumerate(sources):
            me = address(row) ^ address(source)
            for number, tree in enumerate(trees):
                depth, node = 0, me
                while node:
                    depth, node = depth + 1, tree[node]
                mask = sum(1 << d for d in range(4) if tree.get(me ^ (1 << d)) == me)
                pieces.append((depth, index * 4 + number, mask))
        result.append(sorted(pieces))
    return result


def kernel(
    x_ref,
    out_ref,
    high,
    low,
    panel,
    left,
    part,
    fold,
    mid,
    last,
    stage,
    flat,
    in_sem,
    go_sem,
    fold_send,
    fold_recv,
    mid_send,
    mid_recv,
    last_send,
    last_recv,
    out_sem,
    stage_sem,
    *,
    n_row,
    n_col,
):
    p = lax.axis_index("prow")
    q = lax.axis_index("pcol")
    z, c = q // 2, q % 2
    n_block, depth, block = high.shape
    lanes = depth // 128
    per_block = block // 128
    n_stage = n_block * per_block
    n_wave = panel.shape[0]
    n_set = n_wave // (ROWS // PIECE)
    n_step = n_set * SPLIT
    width = part.shape[2]
    half = part.shape[1] // 2
    first_source = n_row - 2
    anchor = n_row * n_block - 2

    x, y = p % 4, p // 4
    near = [
        y * 4 + x + 1 - 2 * (x % 2),
        y * 4 + 3 - x,
        (y + 1 - 2 * (y % 2)) * 4 + x,
        (3 - y) * 4 + x,
    ]
    peer = q + 1 - 2 * c
    up = ((z + 1) % 4) * 2 + c
    down = ((z + 3) % 4) * 2 + c

    def pick(values):
        found = jnp.int32(values[0])
        for k in range(1, n_row):
            found = jnp.where(p == k, jnp.int32(values[k]), found)
        return found

    plan = plans(n_row, (first_source, first_source + 1))
    moves = []
    for k in range(8):
        piece = pick([row[k][1] for row in plan])
        mask = pick([row[k][2] for row in plan])
        late = pick([DELAY[row[k][0]] for row in plan])
        start = pl.multiple_of((piece % 2 * 4 + piece // 2) * (PIECE * lanes), PIECE * lanes)
        turn = [late % TURNS == i for i in range(TURNS)]
        sends = [mask // (1 << d) % 2 == 1 for d in range(4)]
        moves.append((piece, start, late // TURNS, turn, sends))

    ahead = -(-(DELAY[-1] + TURNS * (ROWS // PIECE - 1)) // TURNS)
    size = PIECE * lanes

    def piece_ref(u, start):
        return panel.at[u, pl.ds(start, size), :]

    def stage_copy(n):
        slot = n % SLOTS
        return pltpu.make_async_copy(
            x_ref.at[pl.ds(pl.multiple_of(n * (128 * lanes), 128 * lanes), 128 * lanes), :],
            stage.at[slot],
            stage_sem.at[slot],
        )

    for n in range(SLOTS):
        stage_copy(n).start()

    @pl.when(p >= first_source)
    def _():
        def own(u, _):
            for t in range(4):
                piece = (p - first_source) * 4 + t
                start = pl.multiple_of((t % 2 * 4 + (p - first_source) * 2 + t // 2) * size, size)
                row = (n_block - 1) * block + t * 128 + u * PIECE
                pltpu.make_async_copy(
                    x_ref.at[pl.ds(pl.multiple_of(row * lanes, size), size), :],
                    piece_ref(u, start),
                    in_sem.at[u, piece],
                ).start()
            return 0

        lax.fori_loop(0, n_wave, own, 0)

    barrier = pltpu.get_barrier_semaphore()
    partners = [(row, q) for row in near] + [(p, peer), (p, up), (p, down)]
    for partner in partners:
        pl.semaphore_signal(barrier, inc=1, device_id=partner, device_id_type=MESH)
    pl.semaphore_wait(barrier, len(partners))

    def prepare(n, _):
        slot = n % SLOTS
        stage_copy(n).wait()
        row_id = (
            ((n // per_block) * n_row + p - anchor) * block
            + (n % per_block) * 128
            + lax.broadcasted_iota(jnp.int32, (128, 128), 1)
        )
        for j in range(lanes):
            value = stage[slot, pl.ds(j, 128, stride=lanes), :].T
            first_col = (j // per_block * n_col + q) * block + j % per_block * 128
            if j < per_block:
                col_id = first_col + lax.broadcasted_iota(jnp.int32, (128, 128), 0)
                value = jnp.where(row_id <= col_id, value, 0.0)
            top = value.astype(jnp.bfloat16)
            at = (n // per_block, pl.ds(j * 128, 128), pl.ds(pl.multiple_of(n % per_block * 128, 128), 128))
            high[at] = top
            low[at] = (value - top.astype(jnp.float32)).astype(jnp.bfloat16)

        @pl.when(n + SLOTS < n_stage)
        def _():
            stage_copy(n + SLOTS).start()

        return 0

    def relay(slot, i):
        for piece, start, late, turn, sends in moves:
            u = slot - late

            @pl.when(turn[i] & (u >= 0) & (u < n_wave))
            def _():
                ref = piece_ref(u, start)
                pltpu.make_async_copy(ref, ref, in_sem.at[u, piece]).wait()
                for d in range(4):

                    @pl.when(sends[d])
                    def _():
                        pltpu.make_async_remote_copy(
                            src_ref=ref,
                            dst_ref=ref,
                            send_sem=go_sem.at[piece // 4, d],
                            recv_sem=in_sem.at[u, piece],
                            device_id=(near[d], q),
                            device_id_type=MESH,
                        ).start()

    def split_panel(s):
        row = lax.broadcasted_iota(jnp.int32, (8 * ROWS, 128), 0)
        place_of, within = row // ROWS, row % ROWS
        row_id = (place_of % 4 * 2 + place_of // 4) * 128 + s * ROWS + within
        for j in range(lanes):
            waves = [
                panel[s * (ROWS // PIECE) + w, pl.ds(j, 8 * PIECE, stride=lanes), :]
                for w in range(ROWS // PIECE)
            ]
            value = jnp.concatenate(
                [wave[g * PIECE : g * PIECE + PIECE] for g in range(8) for wave in waves], 0
            )
            if j < per_block:
                col_id = q * block + j * 128 + lax.broadcasted_iota(jnp.int32, (8 * ROWS, 128), 1)
                value = jnp.where(row_id <= col_id, value, 0.0)
            top = value.astype(jnp.bfloat16)
            left[: 8 * ROWS, j * 128 : j * 128 + 128] = top
            left[8 * ROWS :, j * 128 : j * 128 + 128] = (value - top.astype(jnp.float32)).astype(
                jnp.bfloat16
            )

    def fold_copy(t):
        return pltpu.make_async_remote_copy(
            src_ref=part.at[t, pl.ds(pl.multiple_of((1 - c) * half, half), half), :],
            dst_ref=fold.at[t],
            send_sem=fold_send.at[0],
            recv_sem=fold_recv.at[t],
            device_id=(p, peer),
            device_id_type=MESH,
        )

    def rows_of(zone, offset):
        return pl.multiple_of(c * half + zone * ROWS + offset, 8)

    def mid_copy(t, way):
        start = rows_of((z + 2) % 4, way * (ROWS // 2))
        return pltpu.make_async_remote_copy(
            src_ref=part.at[t, pl.ds(start, ROWS // 2), :],
            dst_ref=mid.at[t, way],
            send_sem=mid_send.at[way],
            recv_sem=mid_recv.at[t, way],
            device_id=(p, (up, down)[way]),
            device_id_type=MESH,
        )

    def last_copy(t, way):
        start = rows_of((z + (1, 3)[way]) % 4, 0)
        return pltpu.make_async_remote_copy(
            src_ref=part.at[t, pl.ds(start, ROWS), :],
            dst_ref=last.at[t, way],
            send_sem=last_send.at[way],
            recv_sem=last_recv.at[t, way],
            device_id=(p, (up, down)[way]),
            device_id_type=MESH,
        )

    def out_copy(s):
        rows = ROWS * n_block * per_block
        ref = pl.ds(pl.multiple_of(s * rows, rows), rows)
        return pltpu.make_async_copy(flat.at[ref, :], out_ref.at[ref, :], out_sem.at[0])

    def compute(t, h, i):
        at = h * (n_block // SPLIT) + i
        both = jnp.dot(left[...], high[at], preferred_element_type=jnp.float32)
        rest = jnp.dot(left[: 8 * ROWS], low[at], preferred_element_type=jnp.float32)
        part[t, :, i * block : (i + 1) * block] = both[: 8 * ROWS] + both[8 * ROWS :] + rest

    def add_fold(t):
        fold_copy(t).wait_recv()
        for r in range(0, half, 8):
            at = (t, pl.ds(pl.multiple_of(c * half + r, 8), 8), slice(None))
            part[at] = part[at] + fold[t, r : r + 8, :]
        for way in range(2):
            mid_copy(t, way).start()

    def add_mid(t):
        for way in range(2):
            mid_copy(t, way).wait_recv()
            at = (t, pl.ds(rows_of((z + (1, 3)[way]) % 4, way * (ROWS // 2)), ROWS // 2), slice(None))
            part[at] = part[at] + mid[t, way]
        for way in range(2):
            last_copy(t, way).start()

    def add_last(t):
        for way in range(2):
            last_copy(t, way).wait_recv()
        s, h = t // SPLIT, t % SPLIT
        for j in range(width // 128):
            cols = slice(j * 128, j * 128 + 128)
            value = part[t, pl.ds(rows_of(z, 0), ROWS), cols] + last[t, 0, :, cols] + last[t, 1, :, cols]
            first = s * (ROWS * n_block * per_block) + h * (width // 128) + j
            flat[pl.ds(first, ROWS, stride=n_block * per_block), :] = value

        @pl.when(h == SPLIT - 1)
        def _():
            out_copy(s).start()

    share = -(-n_stage // (ahead * TURNS))

    def fill(slot, _):
        for i in range(TURNS):
            relay(slot, i)
            first = (slot * TURNS + i) * share
            lax.fori_loop(first, jnp.minimum(first + share, n_stage), prepare, 0)
        return 0

    lax.fori_loop(0, ahead, fill, 0)

    def sums(t, work, lag):
        @pl.when((t >= lag) & (t < n_step + lag))
        def _():
            work(t - lag)

    def one_set(s, _):
        for h in range(SPLIT):
            t = s * SPLIT + h
            for i in range(TURNS):
                relay(t + ahead, i)
                if h == 0 and i == 0:
                    split_panel(s)
                compute(t, h, i)
                if i == 1:
                    sums(t, add_fold, LAGS[0])
            fold_copy(t).start()
            sums(t, add_mid, LAGS[1])
            sums(t, add_last, LAGS[2])
        return 0

    lax.fori_loop(0, n_set, one_set, 0)

    def drain(t, _):
        for work, lag in zip((add_fold, add_mid, add_last), LAGS):
            sums(t, work, lag)
        return 0

    lax.fori_loop(n_step, n_step + LAGS[2], drain, 0)
    pltpu.make_async_copy(fold, fold, fold_send.at[0]).wait()
    for way in range(2):
        ref = mid.at[:, way]
        pltpu.make_async_copy(ref, ref, mid_send.at[way]).wait()
        ref = last.at[:, way]
        pltpu.make_async_copy(ref, ref, last_send.at[way]).wait()
    ref = panel.at[:, pl.ds(0, size), :]
    for piece, _, _, _, sends in moves:
        for d in range(4):

            @pl.when(sends[d])
            def _():
                pltpu.make_async_copy(ref, ref, go_sem.at[piece // 4, d]).wait()

    pltpu.make_async_copy(flat, flat, out_sem.at[0]).wait()


def on_device(u_window):
    n_block, _, block, col_blocks, _, _ = u_window.shape
    n_row, n_col = lax.axis_size("prow"), lax.axis_size("pcol")
    depth = col_blocks * block
    lanes = depth // 128
    height = n_block * block
    width = height // SPLIT
    n_set = 128 // ROWS
    n_step = n_set * SPLIT
    n_wave = n_set * (ROWS // PIECE)
    dma = pltpu.SemaphoreType.DMA
    summed = pl.pallas_call(
        functools.partial(kernel, n_row=n_row, n_col=n_col),
        out_shape=jax.ShapeDtypeStruct((2 * block // n_col * (height // 128), 128), jnp.float32),
        in_specs=[pl.BlockSpec(memory_space=pl.ANY)],
        out_specs=pl.BlockSpec(memory_space=pl.ANY),
        scratch_shapes=[
            pltpu.VMEM((n_block, depth, block), jnp.bfloat16),
            pltpu.VMEM((n_block, depth, block), jnp.bfloat16),
            pltpu.VMEM((n_wave, 8 * PIECE * lanes, 128), jnp.float32),
            pltpu.VMEM((16 * ROWS, depth), jnp.bfloat16),
            pltpu.VMEM((n_step, 8 * ROWS, width), jnp.float32),
            pltpu.VMEM((n_step, 4 * ROWS, width), jnp.float32),
            pltpu.VMEM((n_step, 2, ROWS // 2, width), jnp.float32),
            pltpu.VMEM((n_step, 2, ROWS, width), jnp.float32),
            pltpu.VMEM((SLOTS, 128 * lanes, 128), jnp.float32),
            pltpu.VMEM((2 * block // n_col * (height // 128), 128), jnp.float32),
            dma((n_wave, 8)),
            dma((2, 4)),
            dma((1,)),
            dma((n_step,)),
            dma((2,)),
            dma((n_step, 2)),
            dma((2,)),
            dma((n_step, 2)),
            dma((1,)),
            dma((SLOTS,)),
        ],
        compiler_params=pltpu.CompilerParams(
            collective_id=0, has_side_effects=True, vmem_limit_bytes=67043328
        ),
    )(u_window.reshape(height * lanes, 128))
    return summed.reshape(2 * block // n_col, n_block, 1, block)


def solution(mesh):
    placed = (P(None, "prow", None, None, "pcol", None),)
    return jax.shard_map(
        on_device,
        mesh=mesh,
        in_specs=placed,
        out_specs=P("pcol", None, "prow", None),
        check_vma=False,
    )
```

time: 205 us -> 104 us (0.51)
  Pallas kernels: 200 us -> 100 us
    pallas_call x1, Pallas kernels: 200 us -> 100 us  [on_device(): pl.pallas_call(functools.partial(kernel, n_row=n_row, n_col=n_col), out_s...]
    unnamed x0 -> x1, local copies, waits for them, and re-layouts: none -> 3.63 us
    reshape x1 -> x0, local copies, waits for them, and re-layouts: 2.74 us -> none  [on_device(): return summed.reshape(summed.shape[0], n_block, 1, block)]
where the time goes in v2:
time: 104 us
  Pallas kernels  100 us (96%)
  local copies, waits for them, and re-layouts  3.63 us (3%)
    pallas_call x1, Pallas kernels, on_device(): pl.pallas_call(functools.partial(kernel, n_row=n_row, n_col=n_col), out_s...  100 us
    unnamed x1, local copies, waits for them, and re-layouts  3.63 us

profile of v2, /device:TPU:0, one launch (start us, length us, event | category | flops | bytes accessed | tf_op | source)
XLA Modules:
  0.0 103.8 jit_solution(7514797684947421897)
XLA Ops:
  0.0 100.2 %shard_map.17 = f32[3072,128]{1,0:T(8,128)} custom-call(f32[49152,128]{1,0:T(8,128)} %bitcast.2), custom_call_target="tpu_custom_call" | custom-call | tf_op jit(solution)/shard_map/pallas_call | solution.py:379
  100.2 3.6 %copy.5 = f32[128,6,1,512]{3,2,1,0:T(1,128)} copy(f32[128,6,1,512]{3,2,1,0:T(1,128)} %bitcast.3) | data formatting | bytes 3145728

commit v3 on v2

--- a/solution.py
+++ b/solution.py
@@ -11,8 +11,10 @@
 ROWS = 16
 PIECE = 8
 TURNS = 3
-DELAY = (0, 4, 8, 12, 16, 20)
+DELAY = (0, 5, 10, 15, 20, 24)
 SPLIT = 2
+SHIFT = 0
+NEVER = 999
 SLOTS = 3
 LAGS = (1, 2, 4)
 
@@ -44,16 +46,20 @@
             taken.add((parent, node))
     result = []
     for row in range(n_rows):
-        pieces = []
+        into, onward = [], []
         for index, source in enumerate(sources):
             me = address(row) ^ address(source)
             for number, tree in enumerate(trees):
                 depth, node = 0, me
                 while node:
                     depth, node = depth + 1, tree[node]
-                mask = sum(1 << d for d in range(4) if tree.get(me ^ (1 << d)) == me)
-                pieces.append((depth, index * 4 + number, mask))
-        result.append(sorted(pieces))
+                late = DELAY[depth] + SHIFT * index
+                into.append((late, index * 4 + number))
+                for d in range(4):
+                    if tree.get(me ^ (1 << d)) == me:
+                        onward.append((late, index * 4 + number, d))
+        onward = sorted(onward)
+        result.append((sorted(into), onward + [(NEVER, 0, 0)] * (8 - len(onward))))
     return result
 
 
@@ -117,17 +123,27 @@
         return found
 
     plan = plans(n_row, (first_source, first_source + 1))
-    moves = []
+    def schedule(late):
+        turn = [late % TURNS == i for i in range(TURNS)]
+        return late // TURNS, turn
+
+    def offset_of(piece):
+        return pl.multiple_of((piece % 2 * 4 + piece // 2) * (PIECE * lanes), PIECE * lanes)
+
+    into, onward = [], []
     for k in range(8):
-        piece = pick([row[k][1] for row in plan])
-        mask = pick([row[k][2] for row in plan])
-        late = pick([DELAY[row[k][0]] for row in plan])
-        start = pl.multiple_of((piece % 2 * 4 + piece // 2) * (PIECE * lanes), PIECE * lanes)
-        turn = [late % TURNS == i for i in range(TURNS)]
-        sends = [mask // (1 << d) % 2 == 1 for d in range(4)]
-        moves.append((piece, start, late // TURNS, turn, sends))
-
-    ahead = -(-(DELAY[-1] + TURNS * (ROWS // PIECE - 1)) // TURNS)
+        piece = pick([row[0][k][1] for row in plan])
+        late = pick([row[0][k][0] for row in plan])
+        into.append((piece, offset_of(piece), *schedule(late)))
+        piece = pick([row[1][k][1] for row in plan])
+        late = pick([row[1][k][0] for row in plan])
+        axis = pick([row[1][k][2] for row in plan])
+        target = near[0]
+        for d in range(1, 4):
+            target = jnp.where(axis == d, near[d], target)
+        onward.append((piece, offset_of(piece), *schedule(late), target, late < NEVER))
+
+    ahead = -(-(DELAY[-1] + SHIFT + TURNS * (ROWS // PIECE - 1)) // TURNS)
     size = PIECE * lanes
 
     def piece_ref(u, start):
@@ -192,25 +208,28 @@
         return 0
 
     def relay(slot, i):
-        for piece, start, late, turn, sends in moves:
+        for piece, start, late, turn in into:
             u = slot - late
 
             @pl.when(turn[i] & (u >= 0) & (u < n_wave))
             def _():
                 ref = piece_ref(u, start)
                 pltpu.make_async_copy(ref, ref, in_sem.at[u, piece]).wait()
-                for d in range(4):
-
-                    @pl.when(sends[d])
-                    def _():
-                        pltpu.make_async_remote_copy(
-                            src_ref=ref,
-                            dst_ref=ref,
-                            send_sem=go_sem.at[piece // 4, d],
-                            recv_sem=in_sem.at[u, piece],
-                            device_id=(near[d], q),
-                            device_id_type=MESH,
-                        ).start()
+
+        for k, (piece, start, late, turn, target, _) in enumerate(onward):
+            u = slot - late
+
+            @pl.when(turn[i] & (u >= 0) & (u < n_wave))
+            def _():
+                ref = piece_ref(u, start)
+                pltpu.make_async_remote_copy(
+                    src_ref=ref,
+                    dst_ref=ref,
+                    send_sem=go_sem.at[k],
+                    recv_sem=in_sem.at[u, piece],
+                    device_id=(target, q),
+                    device_id_type=MESH,
+                ).start()
 
     def split_panel(s):
         row = lax.broadcasted_iota(jnp.int32, (8 * ROWS, 128), 0)
@@ -355,14 +374,34 @@
         ref = last.at[:, way]
         pltpu.make_async_copy(ref, ref, last_send.at[way]).wait()
     ref = panel.at[:, pl.ds(0, size), :]
-    for piece, _, _, _, sends in moves:
-        for d in range(4):
-
-            @pl.when(sends[d])
-            def _():
-                pltpu.make_async_copy(ref, ref, go_sem.at[piece // 4, d]).wait()
+    for k in range(8):
+
+        @pl.when(onward[k][5])
+        def _():
+            pltpu.make_async_copy(ref, ref, go_sem.at[k]).wait()
 
     pltpu.make_async_copy(flat, flat, out_sem.at[0]).wait()
+
+
+def handed_on(flat):
+    def body(flat_ref, out_ref, sems):
+        rows = flat_ref.shape[0] // 4
+        copies = []
+        for k in range(4):
+            ref = pl.ds(k * rows, rows)
+            copies.append(pltpu.make_async_copy(flat_ref.at[ref, :], out_ref.at[ref, :], sems.at[k]))
+            copies[k].start()
+        for copy in copies:
+            copy.wait()
+
+    return pl.pallas_call(
+        body,
+        out_shape=jax.ShapeDtypeStruct(flat.shape, flat.dtype),
+        in_specs=[pl.BlockSpec(memory_space=pltpu.VMEM)],
+        out_specs=pl.BlockSpec(memory_space=pl.ANY),
+        scratch_shapes=[pltpu.SemaphoreType.DMA((4,))],
+        compiler_params=pltpu.CompilerParams(vmem_limit_bytes=4 * 1024 * 1024),
+    )(flat)
 
 
 def on_device(u_window):
@@ -393,7 +432,7 @@
             pltpu.VMEM((SLOTS, 128 * lanes, 128), jnp.float32),
             pltpu.VMEM((2 * block // n_col * (height // 128), 128), jnp.float32),
             dma((n_wave, 8)),
-            dma((2, 4)),
+            dma((8,)),
             dma((1,)),
             dma((n_step,)),
             dma((2,)),
@@ -407,6 +446,7 @@
             collective_id=0, has_side_effects=True, vmem_limit_bytes=67043328
         ),
     )(u_window.reshape(height * lanes, 128))
+    summed = handed_on(summed)
     return summed.reshape(2 * block // n_col, n_block, 1, block)
 
 

time: 104 us -> 100 us (0.962)
  local copies, waits for them, and re-layouts: 3.63 us -> 1.4 us
  Pallas kernels: 100 us -> 98.8 us
    pallas_call x1, Pallas kernels: 100 us -> 97.7 us  [on_device(): pl.pallas_call(functools.partial(kernel, n_row=n_row, n_col=n_col), out_s...]
    unnamed x1 -> x2, local copies, waits for them, and re-layouts: 3.63 us -> 1.4 us
    pallas_call x0 -> x1, Pallas kernels: none -> 1.17 us  [handed_on(): pl.pallas_call(body, out_shape=jax.ShapeDtypeStruct(flat.shape, flat.dtyp...]
where the time goes in v3:
time: 100 us
  Pallas kernels  98.8 us (99%)
  local copies, waits for them, and re-layouts  1.4 us (1%)
    pallas_call x1, Pallas kernels, on_device(): pl.pallas_call(functools.partial(kernel, n_row=n_row, n_col=n_col), out_s...  97.7 us

profile of v3, /device:TPU:0, one launch (start us, length us, event | category | flops | bytes accessed | tf_op | source)
XLA Modules:
  0.0 100.2 jit_solution(14632118826198147768)
XLA Ops:
  0.0 97.7 %shard_map.17.flat_ref = f32[3072,128]{1,0:T(8,128)} custom-call(f32[49152,128]{1,0:T(8,128)} %bitcast.2), custom_call_target="tpu_custom_call" | custom-call | tf_op jit(solution)/shard_map/pallas_call | solution.py:418
  97.7 0.0 copy-start
  97.7 1.4 %copy-done = f32[3072,128]{1,0:T(8,128)S(1)} copy-done((f32[3072,128]{1,0:T(8,128)S(1)}, f32[3072,128]{1,0:T(8,128)}, u32[]{:S(2)}) %copy-start) | copy-done | bytes 1572888
  99.1 1.2 %shard_map.18 = f32[3072,128]{1,0:T(8,128)} custom-call(f32[3072,128]{1,0:T(8,128)S(1)} %copy-done), custom_call_target="tpu_custom_call" | custom-call | tf_op jit(solution)/shard_map/pallas_call | solution.py:397
Async XLA Ops:
  97.7 1.4 %copy-start = (f32[3072,128]{1,0:T(8,128)S(1)}, f32[3072,128]{1,0:T(8,128)}, u32[]{:S(2)}) copy-start(f32[3072,128]{1,0:T(8,128)} %shard_map.17.flat_ref) | copy-start | bytes 4718596

commit v4 on v3

--- a/solution.py
+++ b/solution.py
@@ -16,7 +16,7 @@
 SHIFT = 0
 NEVER = 999
 SLOTS = 3
-LAGS = (1, 2, 4)
+LAGS = (1, 2, 5)
 
 
 def gray(index):
@@ -116,6 +116,11 @@
     up = ((z + 1) % 4) * 2 + c
     down = ((z + 3) % 4) * 2 + c
 
+    barrier = pltpu.get_barrier_semaphore()
+    partners = [(row, q) for row in near] + [(p, peer), (p, up), (p, down)]
+    for partner in partners:
+        pl.semaphore_signal(barrier, inc=1, device_id=partner, device_id_type=MESH)
+
     def pick(values):
         found = jnp.int32(values[0])
         for k in range(1, n_row):
@@ -176,10 +181,6 @@
 
         lax.fori_loop(0, n_wave, own, 0)
 
-    barrier = pltpu.get_barrier_semaphore()
-    partners = [(row, q) for row in near] + [(p, peer), (p, up), (p, down)]
-    for partner in partners:
-        pl.semaphore_signal(barrier, inc=1, device_id=partner, device_id_type=MESH)
     pl.semaphore_wait(barrier, len(partners))
 
     def prepare(n, _):
@@ -384,23 +385,36 @@
 
 
 def handed_on(flat):
-    def body(flat_ref, out_ref, sems):
-        rows = flat_ref.shape[0] // 4
-        copies = []
-        for k in range(4):
+    parts = 4
+    rows = flat.shape[0] // parts
+
+    def body(flat_ref, out_ref, held, in_sem, out_sem):
+        def take(k):
             ref = pl.ds(k * rows, rows)
-            copies.append(pltpu.make_async_copy(flat_ref.at[ref, :], out_ref.at[ref, :], sems.at[k]))
-            copies[k].start()
-        for copy in copies:
-            copy.wait()
+            return pltpu.make_async_copy(flat_ref.at[ref, :], held.at[ref, :], in_sem.at[k])
+
+        def give(k):
+            ref = pl.ds(k * rows, rows)
+            return pltpu.make_async_copy(held.at[ref, :], out_ref.at[ref, :], out_sem.at[k])
+
+        for k in range(parts):
+            take(k).start()
+        for k in range(parts):
+            take(k).wait()
+            give(k).start()
+        for k in range(parts):
+            give(k).wait()
 
     return pl.pallas_call(
         body,
         out_shape=jax.ShapeDtypeStruct(flat.shape, flat.dtype),
-        in_specs=[pl.BlockSpec(memory_space=pltpu.VMEM)],
+        in_specs=[pl.BlockSpec(memory_space=pl.ANY)],
         out_specs=pl.BlockSpec(memory_space=pl.ANY),
-        scratch_shapes=[pltpu.SemaphoreType.DMA((4,))],
-        compiler_params=pltpu.CompilerParams(vmem_limit_bytes=4 * 1024 * 1024),
+        scratch_shapes=[
+            pltpu.VMEM(flat.shape, flat.dtype),
+            pltpu.SemaphoreType.DMA((parts,)),
+            pltpu.SemaphoreType.DMA((parts,)),
+        ],
     )(flat)
 
 

time: 100 us -> 99.8 us (level)
  local copies, waits for them, and re-layouts: 1.4 us -> 0 us
    unnamed x2 -> x0, local copies, waits for them, and re-layouts: 1.4 us -> none
    pallas_call x1, Pallas kernels: 1.17 us -> 2.2 us  [handed_on(): pl.pallas_call(body, out_shape=jax.ShapeDtypeStruct(flat.shape, flat.dtyp...]
where the time goes in v4:
time: 99.8 us; the launch traced here: 99.6 us
  Pallas kernels  99.6 us (100%)
    pallas_call x1, Pallas kernels, on_device(): pl.pallas_call(functools.partial(kernel, n_row=n_row, n_col=n_col), out_s...  97.4 us
    pallas_call x1, Pallas kernels, handed_on(): pl.pallas_call(body, out_shape=jax.ShapeDtypeStruct(flat.shape, flat.dtyp...  2.2 us

profile of v4, /device:TPU:0, one launch (start us, length us, event | category | flops | bytes accessed | tf_op | source)
XLA Modules:
  0.0 99.6 jit_solution(3224813072254617235)
XLA Ops:
  0.0 97.4 %shard_map.17.flat_ref = f32[3072,128]{1,0:T(8,128)} custom-call(f32[49152,128]{1,0:T(8,128)} %bitcast.2), custom_call_target="tpu_custom_call" | custom-call | tf_op jit(solution)/shard_map/pallas_call | solution.py:432
  97.4 2.2 %shard_map.18 = f32[3072,128]{1,0:T(8,128)} custom-call(f32[3072,128]{1,0:T(8,128)} %shard_map.17.flat_ref), custom_call_target="tpu_custom_call" | custom-call | tf_op jit(solution)/shard_map/pallas_call | solution.py:408

commit v5 on v4

--- a/solution.py
+++ b/solution.py
@@ -162,9 +162,6 @@
             stage_sem.at[slot],
         )
 
-    for n in range(SLOTS):
-        stage_copy(n).start()
-
     @pl.when(p >= first_source)
     def _():
         def own(u, _):
@@ -180,6 +177,9 @@
             return 0
 
         lax.fori_loop(0, n_wave, own, 0)
+
+    for n in range(SLOTS):
+        stage_copy(n).start()
 
     pl.semaphore_wait(barrier, len(partners))
 

time: 99.8 us -> 101 us (1.012)
  no operation moved by 1% of the time
where the time goes in v5:
time: 101 us; the launch traced here: 100 us
  Pallas kernels  100 us (99%)
    pallas_call x1, Pallas kernels, on_device(): pl.pallas_call(functools.partial(kernel, n_row=n_row, n_col=n_col), out_s...  98.2 us
    pallas_call x1, Pallas kernels, handed_on(): pl.pallas_call(body, out_shape=jax.ShapeDtypeStruct(flat.shape, flat.dtyp...  2.2 us

profile of v5, /device:TPU:0, one launch (start us, length us, event | category | flops | bytes accessed | tf_op | source)
XLA Modules:
  0.0 100.4 jit_solution(9456397916074608991)
XLA Ops:
  0.0 98.2 %shard_map.17.flat_ref = f32[3072,128]{1,0:T(8,128)} custom-call(f32[49152,128]{1,0:T(8,128)} %bitcast.2), custom_call_target="tpu_custom_call" | custom-call | tf_op jit(solution)/shard_map/pallas_call | solution.py:432
  98.2 2.2 %shard_map.18 = f32[3072,128]{1,0:T(8,128)} custom-call(f32[3072,128]{1,0:T(8,128)} %shard_map.17.flat_ref), custom_call_target="tpu_custom_call" | custom-call | tf_op jit(solution)/shard_map/pallas_call | solution.py:408
